TPU v7x, 128 devices: a whole 4x4x4 slice. The times are simulated.
128 devices in a mesh: freq: 16 (over y, z_lo, core), feed: 8 (over z_hi, x).
Axes of the slice: x: 4, y: 4, z: 4 (z_hi: 2, z_lo: 2; z = z_hi * 2 + z_lo), core: 2. Of those that a mesh axis runs over, the one named last changes fastest.
Arguments:
- voltages: int32 [64, 2048, 2, 768], P(None, ('feed', 'freq')), may hold values from -127 to 127
- gains: float32 [2, 64, 2048], P(None, None, ('feed', 'freq')), may hold values from -0.06 to 0.06
Outputs:
- visibilities: float32 [64, 2, 2048, 2048], P('freq', None, 'feed')
All inputs are finite; a program needn't handle non-finite values.
Results may differ from a plain program's by a relative error of at most 0.0031.
Values may be sent and summed in bfloat16 or wider, within the bound.
A program may use at most 192 MiB of HBM per device.

v0:
```python
import jax
import jax.numpy as jnp
from jax import lax
from jax.sharding import PartitionSpec as P


def stack_rows(own_rows, samples):
    real_part = own_rows[..., :samples]
    imag_part = own_rows[..., samples:]
    swapped = jnp.concatenate([imag_part, -real_part], axis=-1)
    return jnp.stack([own_rows, swapped], axis=1)


def correlate(stacked, columns, samples):
    product = jnp.einsum("cqrk,cfk->cqrf", stacked, columns, preferred_element_type=jnp.float32)
    return product * (1.0 / samples)


def per_device(voltages, gains):
    channels = voltages.shape[0]
    local_feeds = voltages.shape[1]
    samples = voltages.shape[3]
    freq_count = lax.axis_size("freq")
    owned = channels // freq_count
    volt_real = voltages[:, :, 0, :].astype(jnp.float32)
    volt_imag = voltages[:, :, 1, :].astype(jnp.float32)
    gain_real = gains[0][:, :, None]
    gain_imag = gains[1][:, :, None]
    eq_real = gain_real * volt_real - gain_imag * volt_imag
    eq_imag = gain_real * volt_imag + gain_imag * volt_real
    equalized = jnp.stack([eq_real, eq_imag], axis=2).astype(jnp.bfloat16)
    blocks = equalized.reshape(freq_count, owned, local_feeds, 2 * samples)
    arrived = lax.all_to_all(blocks, "freq", split_axis=0, concat_axis=2, tiled=True)
    own_rows = arrived[0]
    stacked = stack_rows(own_rows, samples)
    return correlate(stacked, lax.all_gather(own_rows, "feed", axis=1, tiled=True), samples)


def solution(mesh):
    in_specs = (P(None, ("feed", "freq"), None, None), P(None, None, ("feed", "freq")))
    out_specs = P("freq", None, "feed", None)
    return jax.shard_map(
        per_device, mesh=mesh, in_specs=in_specs, out_specs=out_specs, check_vma=False
    )
```

profile of v0, /device:TPU:1, one launch (start us, length us, event | category | flops | bytes accessed | tf_op | source)
XLA Modules:
  0.0 372.3 jit_solution(846412902522334450)
XLA Ops:
  6.5 0.0 all-gather.2.cloned.1.call-start
  6.5 0.7 slice_bitcast_fusion.1
  7.3 0.1 copy.7
  7.3 0.1 copy.8
  7.4 12.3 %subtract_convert_fusion = (bf16[64,16,1,768]{3,2,1,0:T(2,128)(2,1)S(1)}, bf16[64,16,1,768]{3,2,1,0:T(2,128)(2,1)S(1)}) fusion(s32[64,16,2,768]{3,2,1,0:T(2,128)} %param.2, f32[64,16]{1,0:T(8,128)S(1)} %copy.8, f32[64,16]{1,0:T(8,128)S(1)} %copy.7), kind=kLoop, calls=%fused_computation.8 | loop fusion | flops 7864320 | bytes 9445376 | tf_op jit(solution)/shard_map/convert
  19.7 8.1 %pad_maximum_fusion.1 = bf16[64,16,2,768]{3,2,1,0:T(2,128)(2,1)} fusion(bf16[64,16,1,768]{3,2,1,0:T(2,128)(2,1)S(1)} %get-tuple-element.6, bf16[64,16,1,768]{3,2,1,0:T(2,128)(2,1)S(1)} %get-tuple-element.5), kind=kLoop, calls=%fused_computation.5 | loop fusion | flops 6291456 | bytes 6291456 | tf_op jit(solution)/shard_map/stack | solution.py:31
  27.8 6.8 %convert_element_type.17 = bf16[16,4,16,1536]{3,2,1,0:T(8,128)(2,1)S(1)} reshape(bf16[64,16,2,768]{3,2,1,0:T(2,128)(2,1)} %pad_maximum_fusion.1) | data formatting | bytes 6291456 | tf_op jit(solution)/shard_map/convert_element_type | solution.py:31
  34.6 44.9 %all_to_all.15 = bf16[16,4,16,1536]{3,2,1,0:T(8,128)(2,1)S(1)} all-to-all(bf16[16,4,16,1536]{3,2,1,0:T(8,128)(2,1)S(1)} %convert_element_type.17), channel_id=1, replica_groups=mesh['freq'=16,'feed'=8] {'freq'}, dimensions={0} | all-to-all | bytes 6291456 | tf_op jit(solution)/shard_map/all_to_all | solution.py:33
  79.5 1.9 copy.9
  81.4 0.0 copy-start
  81.4 0.0 all-gather.2.cloned.1.call-update
  81.4 1.9 copy-done
  83.3 0.2 fusion.5
  83.5 2.0 maximum_bitcast_fusion
  85.5 258.1 %all-gather.2.cloned.1.call-done = bf16[4,2048,1536]{2,1,0:T(8,128)(2,1)} async-done(((bf16[4,256,1536]{2,1,0:T(8,128)(2,1)}), bf16[4,2048,1536]{2,1,0:T(8,128)(2,1)}) %all-gather.2.cloned.1.call-update) | async-done | bytes 25165840 | tf_op jit(solution)/shard_map/all_gather | solution.py:36
  343.6 21.9 %broadcast_multiply_fusion = f32[4,2,256,2048]{3,2,1,0:T(8,128)} fusion(bf16[4,2048,1536]{2,1,0:T(8,128)(2,1)} %all-gather.2.cloned.1.call-done, bf16[4,1,256,1536]{3,2,0,1:T(8,128)(2,1)} %maximum_bitcast_fusion, bf16[4,1,256,1536]{3,2,0,1:T(8,128)(2,1)S(1)} %bitcast.20), kind=kOutput, calls=%fused_computation.2 | convolution fusion | flops 12892241920 | bytes 48234496 | tf_op jit(solution)/shard_map/cqrk,cfk->cqrf/dot_general | solution.py:15
Async XLA Ops:
  6.5 337.0 %all-gather.2.cloned.1.call-start = ((), (), s32[]{:S(2)}) async-start(), calls=%async_computation.1 | async-start | bytes 28311552 | tf_op jit(solution)/shard_map/all_gather | solution.py:36
  81.4 1.9 copy-start
Sparse Core Ops, SparseCore 0:
  81.5 261.9 all-gather.1
where the time goes:
time: 373 us; the launch traced here: 372 us
  waiting for transfers between devices  258 us (69%)
  blocking collectives  44.9 us (12%)
  other arithmetic  22.6 us (6%)
  matrix products  21.9 us (6%)
  between operations  13.4 us (4%)
  local copies, waits for them, and re-layouts  11.4 us (3%)
    all_gather x1, waiting for transfers between devices, per_device(): lax.all_gather(own_rows, 'feed', axis=1, tiled=True)  258 us
    all_to_all x1, blocking collectives, per_device(): lax.all_to_all(blocks, 'freq', split_axis=0, concat_axis=2, tiled=True)  44.9 us
    dot_general x1, matrix products, correlate(): jnp.einsum('cqrk,cfk->cqrf', stacked, columns, preferred_element_type=jnp...  21.9 us
    another operation x1, other arithmetic  12.3 us
    another operation x1, other arithmetic, per_device(): equalized = jnp.stack([eq_real, eq_imag], axis=2).astype(jnp.bfloat16)  8.05 us
  transfers between devices with their start and end apart: 1, of which 1 were waited for; matrix products, arithmetic and copies ran while one was open for 1% of the time, Pallas kernels for 0%

commit v1 on v0

v1 whole, which is shorter than its diff:
```python
import functools

import jax
import jax.numpy as jnp
from jax import lax
from jax.experimental import pallas as pl
from jax.experimental.pallas import tpu as pltpu
from jax.sharding import PartitionSpec as P

MESH = pl.DeviceIdType.MESH
PLANES, PLACES, CORES, ROW = 8, 8, 2, 4


def place():
    freq, feed = lax.axis_index("freq"), lax.axis_index("feed")
    return freq // 2, freq % 2, feed


def chip_at(plane, feed, dx, dy, dz):
    z = (feed // ROW * 2 + plane % 2 + dz) % 4
    y = (plane // 2 + dy) % 4
    x = (feed % ROW + dx) % 4
    return y * 2 + z % 2, z // 2 * ROW + x


def offset_of(step):
    a, b = step // 4 % 4, step % 4
    return a, b, (step // 16 - a - b + 8) % 4


def kernel(volt, gains, arrived, raw, eq, samples, tiles, raw_sem, eq_send, eq_recv, pair_send, pair_recv, out_send, out_recv):
    plane, core, feed = place()
    chans, rows, _, time = volt.shape
    block = rows * PLANES * CORES
    half = block * PLACES // CORES
    me = feed * block + (plane * CORES + core) * rows

    def raw_copy(step):
        p, f = chip_at(plane, feed, *offset_of(step))
        return pltpu.make_async_copy(volt.at[p * PLACES + f], raw.at[step], raw_sem.at[step])

    def start_raw(step, carry):
        raw_copy(step).start()
        return carry

    lax.fori_loop(0, chans, start_raw, 0)

    def eq_copy(step):
        p, f = chip_at(plane, feed, *offset_of(step))
        return pltpu.make_async_remote_copy(
            eq.at[pl.ds(step * rows, rows)], samples.at[pl.ds(me, rows)], eq_send, eq_recv.at[feed],
            device_id={"freq": p * CORES + core, "feed": f}, device_id_type=MESH)

    own_copy = pltpu.make_async_copy(eq.at[pl.ds(0, rows)], samples.at[pl.ds(me, rows)], eq_recv.at[feed])
    lanes = lax.broadcasted_iota(jnp.int32, (rows, 2 * chans), 1)

    def equalize(step, carry):
        raw_copy(step).wait()
        p, f = chip_at(plane, feed, *offset_of(step))
        chan = p * PLACES + f
        g = gains[...]
        gr = jnp.sum(jnp.where(lanes == chan, g, 0.0), axis=1, keepdims=True)
        gi = jnp.sum(jnp.where(lanes == chan + chans, g, 0.0), axis=1, keepdims=True)
        vr = raw[step, :, 0, :].astype(jnp.float32)
        vi = raw[step, :, 1, :].astype(jnp.float32)
        eq[pl.ds(step * rows, rows), :time] = (gr * vr - gi * vi).astype(jnp.bfloat16)
        eq[pl.ds(step * rows, rows), time:] = (gr * vi + gi * vr).astype(jnp.bfloat16)

        @pl.when(step == 1)
        def _():
            own_copy.start()

        @pl.when(step > 1)
        def _():
            eq_copy(step - 1).start()
        return carry

    lax.fori_loop(0, chans, equalize, 0)
    eq_copy(chans - 1).start()

    def pair_copy(f, p):
        at = f * block + (p * CORES + core) * rows
        return pltpu.make_async_remote_copy(
            samples.at[pl.ds(at, rows)], samples.at[pl.ds(at, rows)], pair_send, pair_recv.at[f],
            device_id={"freq": plane * CORES + 1 - core}, device_id_type=MESH)

    def whole(ref, sem):
        return pltpu.make_async_copy(ref, ref, sem)

    def pass_on(f, carry):
        whole(samples.at[pl.ds(0, PLANES * rows)], eq_recv.at[f]).wait()

        def one(p, carry):
            pair_copy(f, p).start()
            return carry
        return lax.fori_loop(0, PLANES, one, carry)

    lax.fori_loop(0, PLACES, pass_on, 0)

    def pair_wait(f, carry):
        whole(samples.at[pl.ds(0, PLANES * rows)], pair_recv.at[f]).wait()
        return carry

    lax.fori_loop(0, PLACES, pair_wait, 0)

    owner = feed // ROW
    slot = feed % ROW
    cols = block
    per_place = half // cols

    def dest(step):
        i = step % PLACES
        dx = i // 2
        dz = i % 2
        return (feed // ROW + dz) % 2 * ROW + (feed % ROW + dx) % 4, step // PLACES

    def tile_ends(step, part):
        to, col = dest(step)
        src = tiles.at[to, part, :, pl.ds(pl.multiple_of(col * cols, cols), cols)]
        dst = arrived.at[slot, part, :, pl.ds(pl.multiple_of(core * half + col * cols, cols), cols)]
        return to, src, dst

    def send(step):
        for part in range(2):
            to, src, dst = tile_ends(step, part)
            far = pltpu.make_async_remote_copy(
                src, dst, out_send, out_recv.at[slot * CORES + core],
                device_id={"freq": plane * CORES + owner, "feed": to}, device_id_type=MESH)
            near = pltpu.make_async_copy(src, dst, out_recv.at[slot * CORES + core])
            here = jnp.logical_and(to == feed, owner == core)

            @pl.when(here)
            def _():
                near.start()

            @pl.when(jnp.logical_not(here))
            def _():
                far.start()

    def correlate(step, carry):
        to, col = dest(step)
        own = samples[pl.ds(pl.multiple_of(to * block, block), block), :]
        turned = jnp.concatenate([own[:, time:], -own[:, :time]], axis=1)
        left = jnp.concatenate([own, turned], axis=0)
        right = samples[pl.ds(pl.multiple_of(core * half + col * cols, cols), cols), :]
        product = lax.dot_general(left, right, (((1,), (1,)), ((), ())), preferred_element_type=jnp.float32)
        product = (product * (1.0 / time)).astype(jnp.bfloat16)
        at = pl.ds(pl.multiple_of(col * cols, cols), cols)
        tiles[to, 0, :, at] = product[:block]
        tiles[to, 1, :, at] = product[block:]

        @pl.when(step > 0)
        def _():
            send(step - 1)
        return carry

    steps = PLACES * per_place
    lax.fori_loop(0, steps, correlate, 0)
    send(steps - 1)

    def landed(i, carry):
        ref = arrived.at[i // CORES, :, :, pl.ds(pl.multiple_of(i % CORES * half, half), half)]
        whole(ref, out_recv.at[i]).wait()
        return carry

    lax.fori_loop(0, ROW * CORES, landed, 0)
    whole(eq.at[pl.ds(0, (chans - 1) * rows)], eq_send).wait()
    whole(samples.at[pl.ds(0, half)], pair_send).wait()

    def sent(i, carry):
        whole(tiles.at[0], out_send).wait()
        return carry

    lax.fori_loop(0, PLACES - 1, sent, 0)

    @pl.when(owner != core)
    def _():
        whole(tiles.at[0], out_send).wait()


def per_device(voltages, gains):
    chans, rows, _, time = voltages.shape
    feeds = rows * PLANES * CORES * PLACES
    block = feeds // PLACES
    owned = chans // (PLANES * CORES)
    flat = gains.transpose(2, 0, 1).reshape(rows, 2 * chans)
    arrived = pl.pallas_call(
        kernel,
        out_shape=jax.ShapeDtypeStruct((owned, 2, block, feeds), jnp.bfloat16),
        in_specs=[pl.BlockSpec(memory_space=pl.ANY), pl.BlockSpec(memory_space=pltpu.VMEM)],
        out_specs=pl.BlockSpec(memory_space=pl.ANY),
        scratch_shapes=[
            pltpu.VMEM((chans, rows, 2, time), jnp.int32),
            pltpu.VMEM((chans * rows, 2 * time), jnp.bfloat16),
            pltpu.VMEM((feeds, 2 * time), jnp.bfloat16),
            pltpu.VMEM((PLACES, 2, block, feeds // CORES), jnp.bfloat16),
            pltpu.SemaphoreType.DMA((chans,)),
            pltpu.SemaphoreType.DMA,
            pltpu.SemaphoreType.DMA((PLACES,)),
            pltpu.SemaphoreType.DMA,
            pltpu.SemaphoreType.DMA((PLACES,)),
            pltpu.SemaphoreType.DMA,
            pltpu.SemaphoreType.DMA((ROW * CORES,)),
        ],
        compiler_params=pltpu.CompilerParams(has_side_effects=True, vmem_limit_bytes=60 * 2**20),
        name="x_engine",
    )(voltages, flat)
    return arrived.astype(jnp.float32)


def solution(mesh):
    in_specs = (P(None, ("feed", "freq"), None, None), P(None, None, ("feed", "freq")))
    out_specs = P("freq", None, "feed", None)
    return jax.shard_map(
        per_device, mesh=mesh, in_specs=in_specs, out_specs=out_specs, check_vma=False
    )
```

time: 373 us -> 193 us (0.52)
  the two profiles are of different devices: /device:TPU:1 before, /device:TPU:92 now
where the time goes in v1:
time: 193 us
  Pallas kernels  180 us (93%)
  other arithmetic  11.7 us (6%)
    pallas_call x1, Pallas kernels, per_device(): pl.pallas_call(kernel, out_shape=jax.ShapeDtypeStruct((owned, 2, block, f...  180 us
    convert_element_type x1, other arithmetic, per_device(): return arrived.astype(jnp.float32)  11.7 us

profile of v1, /device:TPU:92, one launch (start us, length us, event | category | flops | bytes accessed | tf_op | source)
XLA Modules:
  0.0 192.8 jit_solution(17406145350507103668)
XLA Ops:
  0.0 0.7 copy.3
  0.7 0.7 reshape.3.gains
  1.4 179.8 %x_engine.1 = bf16[4,2,256,2048]{3,2,1,0:T(8,128)(2,1)} custom-call(s32[64,16,2,768]{3,2,1,0:T(2,128)} %volt.1, f32[16,128]{1,0:T(8,128)} %reshape.3.gains), custom_call_target="tpu_custom_call" | custom-call | tf_op jit(solution)/shard_map/x_engine/pallas_call | solution.py:187
  181.2 11.7 %convert_element_type.3 = f32[4,2,256,2048]{3,2,1,0:T(8,128)} convert(bf16[4,2,256,2048]{3,2,1,0:T(8,128)(2,1)} %x_engine.1) | non-fusion elementwise | flops 4194304 | bytes 25165824 | tf_op jit(solution)/shard_map/convert_element_type | solution.py:208

commit v2 on v1

--- a/solution.py
+++ b/solution.py
@@ -45,6 +45,20 @@
 
     lax.fori_loop(0, chans, start_raw, 0)
 
+    barrier = pltpu.get_barrier_semaphore()
+
+    def greet(step, carry):
+        p, f = chip_at(plane, feed, *offset_of(step))
+        pl.semaphore_signal(barrier, inc=1, device_id={"freq": p * CORES + core, "feed": f}, device_id_type=MESH)
+        return carry
+
+    def greet_other(f, carry):
+        pl.semaphore_signal(barrier, inc=1, device_id={"freq": plane * CORES + 1 - core, "feed": f}, device_id_type=MESH)
+        return carry
+
+    lax.fori_loop(1, chans, greet, 0)
+    lax.fori_loop(0, PLACES, greet_other, 0)
+
     def eq_copy(step):
         p, f = chip_at(plane, feed, *offset_of(step))
         return pltpu.make_async_remote_copy(
@@ -52,31 +66,29 @@
             device_id={"freq": p * CORES + core, "feed": f}, device_id_type=MESH)
 
     own_copy = pltpu.make_async_copy(eq.at[pl.ds(0, rows)], samples.at[pl.ds(me, rows)], eq_recv.at[feed])
-    lanes = lax.broadcasted_iota(jnp.int32, (rows, 2 * chans), 1)
+    lanes = lax.broadcasted_iota(jnp.int32, (rows, chans), 1)
 
     def equalize(step, carry):
         raw_copy(step).wait()
         p, f = chip_at(plane, feed, *offset_of(step))
         chan = p * PLACES + f
-        g = gains[...]
-        gr = jnp.sum(jnp.where(lanes == chan, g, 0.0), axis=1, keepdims=True)
-        gi = jnp.sum(jnp.where(lanes == chan + chans, g, 0.0), axis=1, keepdims=True)
+        gr = jnp.sum(jnp.where(lanes == chan, gains[0], 0.0), axis=1, keepdims=True)
+        gi = jnp.sum(jnp.where(lanes == chan, gains[1], 0.0), axis=1, keepdims=True)
         vr = raw[step, :, 0, :].astype(jnp.float32)
         vi = raw[step, :, 1, :].astype(jnp.float32)
         eq[pl.ds(step * rows, rows), :time] = (gr * vr - gi * vi).astype(jnp.bfloat16)
         eq[pl.ds(step * rows, rows), time:] = (gr * vi + gi * vr).astype(jnp.bfloat16)
-
-        @pl.when(step == 1)
-        def _():
-            own_copy.start()
-
-        @pl.when(step > 1)
-        def _():
-            eq_copy(step - 1).start()
         return carry
 
     lax.fori_loop(0, chans, equalize, 0)
-    eq_copy(chans - 1).start()
+    pl.semaphore_wait(barrier, chans - 1 + PLACES)
+    own_copy.start()
+
+    def send_eq(step, carry):
+        eq_copy(step).start()
+        return carry
+
+    lax.fori_loop(1, chans, send_eq, 0)
 
     def pair_copy(f, p):
         at = f * block + (p * CORES + core) * rows
@@ -87,42 +99,35 @@
     def whole(ref, sem):
         return pltpu.make_async_copy(ref, ref, sem)
 
-    def pass_on(f, carry):
-        whole(samples.at[pl.ds(0, PLANES * rows)], eq_recv.at[f]).wait()
-
-        def one(p, carry):
-            pair_copy(f, p).start()
+    row_x, row_z = feed % ROW, feed // ROW
+
+    def near_place(dx, dz):
+        return (row_z + dz) % 2 * ROW + (row_x + dx) % ROW
+
+    def exchange(odd):
+        def pass_on(i, carry):
+            f = near_place(odd + i // 2 * 2, i % 2)
+            whole(samples.at[pl.ds(0, PLANES * rows)], eq_recv.at[f]).wait()
+
+            def one(p, carry):
+                pair_copy(f, p).start()
+                return carry
+            return lax.fori_loop(0, PLANES, one, carry)
+
+        def pair_wait(i, carry):
+            f = near_place(odd + i // 2 * 2, i % 2)
+            whole(samples.at[pl.ds(0, PLANES * rows)], pair_recv.at[f]).wait()
             return carry
-        return lax.fori_loop(0, PLANES, one, carry)
-
-    lax.fori_loop(0, PLACES, pass_on, 0)
-
-    def pair_wait(f, carry):
-        whole(samples.at[pl.ds(0, PLANES * rows)], pair_recv.at[f]).wait()
-        return carry
-
-    lax.fori_loop(0, PLACES, pair_wait, 0)
-
-    owner = feed // ROW
-    slot = feed % ROW
-    cols = block
-    per_place = half // cols
-
-    def dest(step):
-        i = step % PLACES
-        dx = i // 2
-        dz = i % 2
-        return (feed // ROW + dz) % 2 * ROW + (feed % ROW + dx) % 4, step // PLACES
-
-    def tile_ends(step, part):
-        to, col = dest(step)
-        src = tiles.at[to, part, :, pl.ds(pl.multiple_of(col * cols, cols), cols)]
-        dst = arrived.at[slot, part, :, pl.ds(pl.multiple_of(core * half + col * cols, cols), cols)]
-        return to, src, dst
-
-    def send(step):
+
+        lax.fori_loop(0, PLACES // 2, pass_on, 0)
+        lax.fori_loop(0, PLACES // 2, pair_wait, 0)
+
+    owner, slot, cols = row_z, row_x, block
+
+    def send(to, col):
         for part in range(2):
-            to, src, dst = tile_ends(step, part)
+            src = tiles.at[to, part, :, pl.ds(pl.multiple_of(col * cols, cols), cols)]
+            dst = arrived.at[slot, part, :, pl.ds(pl.multiple_of(core * half + col * cols, cols), cols)]
             far = pltpu.make_async_remote_copy(
                 src, dst, out_send, out_recv.at[slot * CORES + core],
                 device_id={"freq": plane * CORES + owner, "feed": to}, device_id_type=MESH)
@@ -137,8 +142,7 @@
             def _():
                 far.start()
 
-    def correlate(step, carry):
-        to, col = dest(step)
+    def correlate(to, col):
         own = samples[pl.ds(pl.multiple_of(to * block, block), block), :]
         turned = jnp.concatenate([own[:, time:], -own[:, :time]], axis=1)
         left = jnp.concatenate([own, turned], axis=0)
@@ -149,14 +153,34 @@
         tiles[to, 0, :, at] = product[:block]
         tiles[to, 1, :, at] = product[block:]
 
-        @pl.when(step > 0)
-        def _():
-            send(step - 1)
-        return carry
-
-    steps = PLACES * per_place
-    lax.fori_loop(0, steps, correlate, 0)
-    send(steps - 1)
+    def tile_loop(steps, tile):
+        def one(step, carry):
+            correlate(*tile(step))
+
+            @pl.when(step > 0)
+            def _():
+                send(*tile(step - 1))
+            return carry
+
+        lax.fori_loop(0, steps, one, 0)
+        send(*tile(steps - 1))
+
+    def even_tile(step):
+        i = step % 4
+        return near_place(2 - i // 2 * 2, 1 - i % 2), (row_x + step // 4 * 2) % ROW
+
+    def other_tile(step):
+        turn, i = step // 6, step % 6
+        odd = i < 4
+        dx = jnp.where(odd, 3 - i % 2 * 2, 2 - turn % 2 * 2)
+        dz = jnp.where(odd, 1 - i // 2, 5 - i)
+        col = jnp.where(odd, turn, 1 + turn // 2 * 2)
+        return near_place(dx, dz), (row_x + col) % ROW
+
+    exchange(0)
+    exchange(1)
+    tile_loop(8, even_tile)
+    tile_loop(24, other_tile)
 
     def landed(i, carry):
         ref = arrived.at[i // CORES, :, :, pl.ds(pl.multiple_of(i % CORES * half, half), half)]
@@ -183,7 +207,6 @@
     feeds = rows * PLANES * CORES * PLACES
     block = feeds // PLACES
     owned = chans // (PLANES * CORES)
-    flat = gains.transpose(2, 0, 1).reshape(rows, 2 * chans)
     arrived = pl.pallas_call(
         kernel,
         out_shape=jax.ShapeDtypeStruct((owned, 2, block, feeds), jnp.bfloat16),
@@ -202,9 +225,9 @@
             pltpu.SemaphoreType.DMA,
             pltpu.SemaphoreType.DMA((ROW * CORES,)),
         ],
-        compiler_params=pltpu.CompilerParams(has_side_effects=True, vmem_limit_bytes=60 * 2**20),
+        compiler_params=pltpu.CompilerParams(collective_id=0, has_side_effects=True, vmem_limit_bytes=60 * 2**20),
         name="x_engine",
-    )(voltages, flat)
+    )(voltages, gains.transpose(0, 2, 1))
     return arrived.astype(jnp.float32)
 
 

time: 193 us -> 179 us (0.927)
  the two profiles are of different devices: /device:TPU:92 before, /device:TPU:4 now
where the time goes in v2:
time: 179 us
  Pallas kernels  167 us (93%)
  other arithmetic  11.7 us (7%)
    pallas_call x1, Pallas kernels, per_device(): pl.pallas_call(kernel, out_shape=jax.ShapeDtypeStruct((owned, 2, block, f...  167 us
    convert_element_type x1, other arithmetic, per_device(): return arrived.astype(jnp.float32)  11.7 us

profile of v2, /device:TPU:4, one launch (start us, length us, event | category | flops | bytes accessed | tf_op | source)
XLA Modules:
  0.0 179.1 jit_solution(3223282303136351038)
XLA Ops:
  0.0 167.4 %x_engine.1 = bf16[4,2,256,2048]{3,2,1,0:T(8,128)(2,1)} custom-call(s32[64,16,2,768]{3,2,1,0:T(2,128)} %volt.1, f32[2,16,64]{2,1,0:T(8,128)} %bitcast.1), custom_call_target="tpu_custom_call" | custom-call | tf_op jit(solution)/shard_map/x_engine/pallas_call | solution.py:210
  167.4 11.7 %convert_element_type.3 = f32[4,2,256,2048]{3,2,1,0:T(8,128)} convert(bf16[4,2,256,2048]{3,2,1,0:T(8,128)(2,1)} %x_engine.1) | non-fusion elementwise | flops 4194304 | bytes 25165824 | tf_op jit(solution)/shard_map/convert_element_type | solution.py:231

commit v3 on v2

--- a/solution.py
+++ b/solution.py
@@ -11,6 +11,38 @@
 PLANES, PLACES, CORES, ROW = 8, 8, 2, 4
 
 
+RELAYS = (
+    ((0, 3), (2, 1)), ((0, 1), (2, 1)), ((0, 2), (2, 1)), ((0, 1), (1, 1)), ((0, 3), (3, 1)), ((0, 1), (2, 0)), ((0, 3), (2, 0)),
+    ((1, 0), (2, 1)), ((1, 1), (2, 1)), ((1, 3), (2, 1)), ((1, 0), (1, 1)), ((1, 0), (3, 1)),
+)
+TILES = (
+    ((1, 0, 2), (3, 0, 2), (2, 1, 0), (1, 1, 0), (3, 1, 0), (2, 0, 0), (0, 1, 0), (1, 0, 0), (3, 0, 0), (0, 0, 0), (1, 1, 2),
+     (3, 1, 2), (0, 1, 1), (2, 0, 2), (1, 0, 1), (3, 0, 1), (0, 0, 1), (1, 1, 3), (3, 1, 1), (0, 1, 2), (1, 0, 3), (3, 0, 3),
+     (0, 1, 3), (0, 0, 2), (0, 0, 3)),
+    ((1, 0, 2), (3, 0, 2), (0, 1, 2), (2, 0, 2), (1, 1, 2), (3, 1, 2), (0, 1, 1), (1, 0, 1), (3, 0, 3), (0, 1, 3), (2, 1, 2),
+     (1, 1, 1), (3, 1, 1), (2, 0, 0), (0, 1, 0), (1, 0, 0), (3, 0, 0), (0, 0, 0), (1, 1, 3), (3, 1, 3), (2, 0, 1), (1, 0, 3),
+     (3, 0, 1), (0, 0, 1), (2, 0, 3), (0, 0, 2), (0, 0, 3)),
+)
+
+
+def pick(table, step):
+    out = []
+    for column in zip(*table):
+        value = jnp.int32(column[0])
+        for n in range(1, len(column)):
+            value = jnp.where(step == n, column[n], value)
+        out.append(value)
+    return out
+
+
+def relayed(giver_dz, giver_dx, taker_dx, taker_dz):
+    hit = jnp.bool_(False)
+    for (az, ax), (bx, bz) in RELAYS:
+        same = (giver_dz == az) & (giver_dx == ax) & (taker_dx == bx) & (taker_dz == bz)
+        hit = hit | same
+    return hit
+
+
 def place():
     freq, feed = lax.axis_index("freq"), lax.axis_index("feed")
     return freq // 2, freq % 2, feed
@@ -28,7 +60,7 @@
     return a, b, (step // 16 - a - b + 8) % 4
 
 
-def kernel(volt, gains, arrived, raw, eq, samples, tiles, raw_sem, eq_send, eq_recv, pair_send, pair_recv, out_send, out_recv):
+def kernel(volt, gains, arrived, raw, eq, samples, tiles, raw_sem, eq_send, eq_recv, pair_send, pair_recv, out_send, out_recv, relay_send):
     plane, core, feed = place()
     chans, rows, _, time = volt.shape
     block = rows * PLANES * CORES
@@ -129,9 +161,9 @@
             src = tiles.at[to, part, :, pl.ds(pl.multiple_of(col * cols, cols), cols)]
             dst = arrived.at[slot, part, :, pl.ds(pl.multiple_of(core * half + col * cols, cols), cols)]
             far = pltpu.make_async_remote_copy(
-                src, dst, out_send, out_recv.at[slot * CORES + core],
+                src, dst, out_send, out_recv.at[slot, core * ROW + col],
                 device_id={"freq": plane * CORES + owner, "feed": to}, device_id_type=MESH)
-            near = pltpu.make_async_copy(src, dst, out_recv.at[slot * CORES + core])
+            near = pltpu.make_async_copy(src, dst, out_recv.at[slot, core * ROW + col])
             here = jnp.logical_and(to == feed, owner == core)
 
             @pl.when(here)
@@ -165,41 +197,81 @@
         lax.fori_loop(0, steps, one, 0)
         send(*tile(steps - 1))
 
-    def even_tile(step):
-        i = step % 4
-        return near_place(2 - i // 2 * 2, 1 - i % 2), (row_x + step // 4 * 2) % ROW
-
-    def other_tile(step):
-        turn, i = step // 6, step % 6
-        odd = i < 4
-        dx = jnp.where(odd, 3 - i % 2 * 2, 2 - turn % 2 * 2)
-        dz = jnp.where(odd, 1 - i // 2, 5 - i)
-        col = jnp.where(odd, turn, 1 + turn // 2 * 2)
+    far_side = (core + row_z) % 2
+    steps = len(TILES[0]) + far_side * (len(TILES[1]) - len(TILES[0]))
+
+    def tile(step):
+        close, far = pick(TILES[0], step), pick(TILES[1], step)
+        dx, dz, col = (jnp.where(far_side == 1, v, u) for u, v in zip(close, far))
         return near_place(dx, dz), (row_x + col) % ROW
 
     exchange(0)
     exchange(1)
-    tile_loop(8, even_tile)
-    tile_loop(24, other_tile)
+    tile_loop(steps, tile)
+
+    def columns(source, f):
+        return arrived.at[source, :, :, pl.ds(pl.multiple_of(f * cols, cols), cols)]
+
+    near_relays = tuple((ax, bx, bz) for (az, ax), (bx, bz) in RELAYS if az == 0)
+    far_relays = tuple((ax, bx, bz) for (az, ax), (bx, bz) in RELAYS if az == 1)
+    relays = len(near_relays) + far_side * (len(far_relays) - len(near_relays))
+
+    def hand_on(n, carry):
+        ax, bx, bz = (jnp.where(far_side == 1, v, u) for u, v in zip(pick(near_relays, n), pick(far_relays, n)))
+        source = (row_x - ax + ROW) % ROW
+        to = (core + bz) % 2 * ROW + (source + bx) % ROW
+        whole(columns(source, to), out_recv.at[source, to]).wait()
+        pltpu.make_async_remote_copy(
+            columns(source, to), columns(source, feed), relay_send, out_recv.at[source, feed],
+            device_id={"freq": plane * CORES + core, "feed": to}, device_id_type=MESH).start()
+        return carry
+
+    lax.fori_loop(0, relays, hand_on, 0)
 
     def landed(i, carry):
-        ref = arrived.at[i // CORES, :, :, pl.ds(pl.multiple_of(i % CORES * half, half), half)]
-        whole(ref, out_recv.at[i]).wait()
-        return carry
-
-    lax.fori_loop(0, ROW * CORES, landed, 0)
+        source, f = i // PLACES, i % PLACES
+        seen = relayed(far_side, (row_x - source + ROW) % ROW, (f % ROW - source + ROW) % ROW, (f // ROW + core) % 2)
+
+        @pl.when(jnp.logical_not(seen))
+        def _():
+            whole(columns(source, f), out_recv.at[source, f]).wait()
+        return carry
+
+    lax.fori_loop(0, ROW * PLACES, landed, 0)
     whole(eq.at[pl.ds(0, (chans - 1) * rows)], eq_send).wait()
     whole(samples.at[pl.ds(0, half)], pair_send).wait()
+    one_tile = tiles.at[0, :, :, pl.ds(0, cols)]
 
     def sent(i, carry):
-        whole(tiles.at[0], out_send).wait()
-        return carry
-
-    lax.fori_loop(0, PLACES - 1, sent, 0)
-
-    @pl.when(owner != core)
-    def _():
-        whole(tiles.at[0], out_send).wait()
+        whole(one_tile, out_send).wait()
+        return carry
+
+    lax.fori_loop(0, steps - jnp.where(owner == core, ROW, 0), sent, 0)
+
+    def handed(i, carry):
+        whole(one_tile, relay_send).wait()
+        return carry
+
+    lax.fori_loop(0, relays, handed, 0)
+
+
+def finish(arrived, out):
+    _, core, feed = place()
+    source, width = pl.program_id(0), out.shape[2]
+    for n in range(out.shape[3] // width):
+        f = pl.program_id(1) * (out.shape[3] // width) + n
+        turned = relayed((f // ROW + core) % 2, (f % ROW - source + ROW) % ROW,
+                         (feed % ROW - source + ROW) % ROW, (feed // ROW + core) % 2)
+        at = slice(n * width, (n + 1) * width)
+
+        @pl.when(turned)
+        def _():
+            out[0, 0, :, at] = arrived[0, 0, :, at].astype(jnp.float32).T
+            out[0, 1, :, at] = -arrived[0, 1, :, at].astype(jnp.float32).T
+
+        @pl.when(jnp.logical_not(turned))
+        def _():
+            out[0, :, :, at] = arrived[0, :, :, at].astype(jnp.float32)
 
 
 def per_device(voltages, gains):
@@ -223,12 +295,21 @@
             pltpu.SemaphoreType.DMA,
             pltpu.SemaphoreType.DMA((PLACES,)),
             pltpu.SemaphoreType.DMA,
-            pltpu.SemaphoreType.DMA((ROW * CORES,)),
+            pltpu.SemaphoreType.DMA((ROW, PLACES)),
+            pltpu.SemaphoreType.DMA,
         ],
         compiler_params=pltpu.CompilerParams(collective_id=0, has_side_effects=True, vmem_limit_bytes=60 * 2**20),
         name="x_engine",
     )(voltages, gains.transpose(0, 2, 1))
-    return arrived.astype(jnp.float32)
+    spec = pl.BlockSpec((1, 2, block, feeds // 2), lambda i, j: (i, 0, 0, j))
+    return pl.pallas_call(
+        finish,
+        out_shape=jax.ShapeDtypeStruct(arrived.shape, jnp.float32),
+        grid=(owned, 2),
+        in_specs=[spec],
+        out_specs=spec,
+        name="widen",
+    )(arrived)
 
 
 def solution(mesh):

time: 179 us -> 163 us (0.911)
  the two profiles are of different devices: /device:TPU:4 before, /device:TPU:1 now
where the time goes in v3:
time: 163 us; the launch traced here: 162 us
  Pallas kernels  162 us (99%)
    pallas_call x1, Pallas kernels, per_device(): pl.pallas_call(kernel, out_shape=jax.ShapeDtypeStruct((owned, 2, block, f...  151 us
    pallas_call x1, Pallas kernels, per_device(): pl.pallas_call(finish, out_shape=jax.ShapeDtypeStruct(arrived.shape, jnp....  11.5 us

profile of v3, /device:TPU:1, one launch (start us, length us, event | category | flops | bytes accessed | tf_op | source)
XLA Modules:
  0.0 162.4 jit_solution(12575041186717342466)
XLA Ops:
  0.0 150.8 %x_engine.1.arrived = bf16[4,2,256,2048]{3,2,1,0:T(8,128)(2,1)} custom-call(s32[64,16,2,768]{3,2,1,0:T(2,128)} %volt.1, f32[2,16,64]{2,1,0:T(8,128)} %bitcast.1), custom_call_target="tpu_custom_call" | custom-call | tf_op jit(solution)/shard_map/x_engine/pallas_call | solution.py:282
  150.8 11.5 %widen.1 = f32[4,2,256,2048]{3,2,1,0:T(8,128)} custom-call(bf16[4,2,256,2048]{3,2,1,0:T(8,128)(2,1)} %x_engine.1.arrived), custom_call_target="tpu_custom_call" | custom-call | tf_op jit(solution)/shard_map/widen/pallas_call | solution.py:305

commit v4 on v3

--- a/solution.py
+++ b/solution.py
@@ -16,12 +16,8 @@
     ((1, 0), (2, 1)), ((1, 1), (2, 1)), ((1, 3), (2, 1)), ((1, 0), (1, 1)), ((1, 0), (3, 1)),
 )
 TILES = (
-    ((1, 0, 2), (3, 0, 2), (2, 1, 0), (1, 1, 0), (3, 1, 0), (2, 0, 0), (0, 1, 0), (1, 0, 0), (3, 0, 0), (0, 0, 0), (1, 1, 2),
-     (3, 1, 2), (0, 1, 1), (2, 0, 2), (1, 0, 1), (3, 0, 1), (0, 0, 1), (1, 1, 3), (3, 1, 1), (0, 1, 2), (1, 0, 3), (3, 0, 3),
-     (0, 1, 3), (0, 0, 2), (0, 0, 3)),
-    ((1, 0, 2), (3, 0, 2), (0, 1, 2), (2, 0, 2), (1, 1, 2), (3, 1, 2), (0, 1, 1), (1, 0, 1), (3, 0, 3), (0, 1, 3), (2, 1, 2),
-     (1, 1, 1), (3, 1, 1), (2, 0, 0), (0, 1, 0), (1, 0, 0), (3, 0, 0), (0, 0, 0), (1, 1, 3), (3, 1, 3), (2, 0, 1), (1, 0, 3),
-     (3, 0, 1), (0, 0, 1), (2, 0, 3), (0, 0, 2), (0, 0, 3)),
+    ((1, 0, 2), (3, 0, 2), (0, 1, 0), (1, 1, 0), (3, 1, 0), (2, 0, 0), (1, 0, 0), (3, 0, 0), (0, 1, 1), (1, 1, 2), (3, 1, 1), (2, 1, 0), (1, 0, 1), (3, 0, 1), (0, 1, 2), (2, 0, 2), (1, 1, 3), (3, 1, 2), (1, 0, 3), (3, 0, 3), (0, 1, 3), (0, 0, 0), (0, 0, 1), (0, 0, 2), (0, 0, 3)),
+    ((1, 0, 1), (3, 0, 2), (0, 1, 1), (2, 0, 2), (1, 1, 2), (3, 1, 2), (1, 0, 2), (3, 0, 3), (0, 1, 2), (2, 0, 0), (0, 1, 3), (1, 1, 1), (3, 1, 1), (2, 1, 2), (1, 0, 0), (3, 0, 0), (2, 0, 1), (1, 1, 3), (3, 1, 3), (1, 0, 3), (3, 0, 1), (0, 1, 0), (2, 0, 3), (0, 0, 0), (0, 0, 1), (0, 0, 2), (0, 0, 3)),
 )
 
 
@@ -75,7 +71,6 @@
         raw_copy(step).start()
         return carry
 
-    lax.fori_loop(0, chans, start_raw, 0)
 
     barrier = pltpu.get_barrier_semaphore()
 
@@ -90,14 +85,15 @@
 
     lax.fori_loop(1, chans, greet, 0)
     lax.fori_loop(0, PLACES, greet_other, 0)
+    lax.fori_loop(0, chans, start_raw, 0)
 
     def eq_copy(step):
         p, f = chip_at(plane, feed, *offset_of(step))
         return pltpu.make_async_remote_copy(
-            eq.at[pl.ds(step * rows, rows)], samples.at[pl.ds(me, rows)], eq_send, eq_recv.at[feed],
+            eq.at[pl.ds(step * rows, rows)], samples.at[pl.ds(me, rows)], eq_send, eq_recv.at[feed, plane],
             device_id={"freq": p * CORES + core, "feed": f}, device_id_type=MESH)
 
-    own_copy = pltpu.make_async_copy(eq.at[pl.ds(0, rows)], samples.at[pl.ds(me, rows)], eq_recv.at[feed])
+    own_copy = pltpu.make_async_copy(eq.at[pl.ds(0, rows)], samples.at[pl.ds(me, rows)], eq_recv.at[feed, plane])
     lanes = lax.broadcasted_iota(jnp.int32, (rows, chans), 1)
 
     def equalize(step, carry):
@@ -125,7 +121,7 @@
     def pair_copy(f, p):
         at = f * block + (p * CORES + core) * rows
         return pltpu.make_async_remote_copy(
-            samples.at[pl.ds(at, rows)], samples.at[pl.ds(at, rows)], pair_send, pair_recv.at[f],
+            samples.at[pl.ds(at, rows)], samples.at[pl.ds(at, rows)], pair_send, pair_recv,
             device_id={"freq": plane * CORES + 1 - core}, device_id_type=MESH)
 
     def whole(ref, sem):
@@ -136,23 +132,12 @@
     def near_place(dx, dz):
         return (row_z + dz) % 2 * ROW + (row_x + dx) % ROW
 
-    def exchange(odd):
-        def pass_on(i, carry):
-            f = near_place(odd + i // 2 * 2, i % 2)
-            whole(samples.at[pl.ds(0, PLANES * rows)], eq_recv.at[f]).wait()
-
-            def one(p, carry):
-                pair_copy(f, p).start()
-                return carry
-            return lax.fori_loop(0, PLANES, one, carry)
-
-        def pair_wait(i, carry):
-            f = near_place(odd + i // 2 * 2, i % 2)
-            whole(samples.at[pl.ds(0, PLANES * rows)], pair_recv.at[f]).wait()
-            return carry
-
-        lax.fori_loop(0, PLACES // 2, pass_on, 0)
-        lax.fori_loop(0, PLACES // 2, pair_wait, 0)
+    def pass_on(step, carry):
+        dx, dy, dz = offset_of(step)
+        p, f = chip_at(plane, feed, 4 - dx, 4 - dy, 4 - dz)
+        whole(samples.at[pl.ds(0, rows)], eq_recv.at[f, p]).wait()
+        pair_copy(f, p).start()
+        return carry
 
     owner, slot, cols = row_z, row_x, block
 
@@ -205,8 +190,8 @@
         dx, dz, col = (jnp.where(far_side == 1, v, u) for u, v in zip(close, far))
         return near_place(dx, dz), (row_x + col) % ROW
 
-    exchange(0)
-    exchange(1)
+    lax.fori_loop(0, chans, pass_on, 0)
+    whole(samples.at[pl.ds(0, half)], pair_recv).wait()
     tile_loop(steps, tile)
 
     def columns(source, f):
@@ -263,15 +248,16 @@
         turned = relayed((f // ROW + core) % 2, (f % ROW - source + ROW) % ROW,
                          (feed % ROW - source + ROW) % ROW, (feed // ROW + core) % 2)
         at = slice(n * width, (n + 1) * width)
+        took = pl.ds(pl.multiple_of(f * width, width), width)
 
         @pl.when(turned)
         def _():
-            out[0, 0, :, at] = arrived[0, 0, :, at].astype(jnp.float32).T
-            out[0, 1, :, at] = -arrived[0, 1, :, at].astype(jnp.float32).T
+            out[0, 0, :, at] = arrived[source, 0, :, took].astype(jnp.float32).T
+            out[0, 1, :, at] = -arrived[source, 1, :, took].astype(jnp.float32).T
 
         @pl.when(jnp.logical_not(turned))
         def _():
-            out[0, :, :, at] = arrived[0, :, :, at].astype(jnp.float32)
+            out[0, :, :, at] = arrived[source, :, :, took].astype(jnp.float32)
 
 
 def per_device(voltages, gains):
@@ -281,9 +267,9 @@
     owned = chans // (PLANES * CORES)
     arrived = pl.pallas_call(
         kernel,
-        out_shape=jax.ShapeDtypeStruct((owned, 2, block, feeds), jnp.bfloat16),
-        in_specs=[pl.BlockSpec(memory_space=pl.ANY), pl.BlockSpec(memory_space=pltpu.VMEM)],
-        out_specs=pl.BlockSpec(memory_space=pl.ANY),
+        out_shape=pltpu.VMEM((owned, 2, block, feeds), jnp.bfloat16),
+        in_specs=[pl.BlockSpec(memory_space=pltpu.HBM), pl.BlockSpec(memory_space=pltpu.VMEM)],
+        out_specs=pl.BlockSpec(memory_space=pltpu.VMEM),
         scratch_shapes=[
             pltpu.VMEM((chans, rows, 2, time), jnp.int32),
             pltpu.VMEM((chans * rows, 2 * time), jnp.bfloat16),
@@ -291,14 +277,14 @@
             pltpu.VMEM((PLACES, 2, block, feeds // CORES), jnp.bfloat16),
             pltpu.SemaphoreType.DMA((chans,)),
             pltpu.SemaphoreType.DMA,
-            pltpu.SemaphoreType.DMA((PLACES,)),
-            pltpu.SemaphoreType.DMA,
-            pltpu.SemaphoreType.DMA((PLACES,)),
+            pltpu.SemaphoreType.DMA((PLACES, PLANES)),
+            pltpu.SemaphoreType.DMA,
+            pltpu.SemaphoreType.DMA,
             pltpu.SemaphoreType.DMA,
             pltpu.SemaphoreType.DMA((ROW, PLACES)),
             pltpu.SemaphoreType.DMA,
         ],
-        compiler_params=pltpu.CompilerParams(collective_id=0, has_side_effects=True, vmem_limit_bytes=60 * 2**20),
+        compiler_params=pltpu.CompilerParams(collective_id=0, has_side_effects=True, vmem_limit_bytes=45 * 2**20),
         name="x_engine",
     )(voltages, gains.transpose(0, 2, 1))
     spec = pl.BlockSpec((1, 2, block, feeds // 2), lambda i, j: (i, 0, 0, j))
@@ -306,8 +292,9 @@
         finish,
         out_shape=jax.ShapeDtypeStruct(arrived.shape, jnp.float32),
         grid=(owned, 2),
-        in_specs=[spec],
+        in_specs=[pl.BlockSpec(memory_space=pltpu.VMEM)],
         out_specs=spec,
+        compiler_params=pltpu.CompilerParams(vmem_limit_bytes=16 * 2**20),
         name="widen",
     )(arrived)
 

time: 163 us -> 150 us (0.920)
  Pallas kernels: 162 us -> 150 us
    pallas_call x1, Pallas kernels: 151 us -> 142 us  [per_device(): pl.pallas_call(kernel, out_shape=pltpu.VMEM((owned, 2, block, feeds), jnp...]
    pallas_call x1, Pallas kernels: 11.5 us -> 7.81 us  [per_device(): pl.pallas_call(finish, out_shape=jax.ShapeDtypeStruct(arrived.shape, jnp....]
where the time goes in v4:
time: 150 us
  Pallas kernels  150 us (100%)
    pallas_call x1, Pallas kernels, per_device(): pl.pallas_call(kernel, out_shape=pltpu.VMEM((owned, 2, block, feeds), jnp...  142 us
    pallas_call x1, Pallas kernels, per_device(): pl.pallas_call(finish, out_shape=jax.ShapeDtypeStruct(arrived.shape, jnp....  7.81 us

profile of v4, /device:TPU:1, one launch (start us, length us, event | category | flops | bytes accessed | tf_op | source)
XLA Modules:
  0.0 150.3 jit_solution(13889201095855686772)
XLA Ops:
  0.0 0.0 copy-start
  0.0 0.7 copy-done
  0.7 141.8 %x_engine.1.arrived = bf16[4,2,256,2048]{3,2,1,0:T(8,128)(2,1)S(1)} custom-call(s32[64,16,2,768]{3,2,1,0:T(2,128)} %volt.1, f32[2,16,64]{2,1,0:T(8,128)S(1)} %bitcast.1), custom_call_target="tpu_custom_call" | custom-call | tf_op jit(solution)/shard_map/x_engine/pallas_call | solution.py:268
  142.5 7.8 %widen.1 = f32[4,2,256,2048]{3,2,1,0:T(8,128)} custom-call(bf16[4,2,256,2048]{3,2,1,0:T(8,128)(2,1)S(1)} %x_engine.1.arrived), custom_call_target="tpu_custom_call" | custom-call | tf_op jit(solution)/shard_map/widen/pallas_call | solution.py:291
Async XLA Ops:
  0.0 0.7 copy-start

commit v5 on v4

--- a/solution.py
+++ b/solution.py
@@ -108,7 +108,7 @@
         eq[pl.ds(step * rows, rows), time:] = (gr * vi + gi * vr).astype(jnp.bfloat16)
         return carry
 
-    lax.fori_loop(0, chans, equalize, 0)
+    lax.fori_loop(0, 24, equalize, 0)
     pl.semaphore_wait(barrier, chans - 1 + PLACES)
     own_copy.start()
 
@@ -116,7 +116,18 @@
         eq_copy(step).start()
         return carry
 
-    lax.fori_loop(1, chans, send_eq, 0)
+    lax.fori_loop(1, 24, send_eq, 0)
+
+    def equalize_and_send(step, carry):
+        equalize(step, carry)
+
+        @pl.when(step > 24)
+        def _():
+            eq_copy(step - 1).start()
+        return carry
+
+    lax.fori_loop(24, chans, equalize_and_send, 0)
+    eq_copy(chans - 1).start()
 
     def pair_copy(f, p):
         at = f * block + (p * CORES + core) * rows
@@ -141,23 +152,35 @@
 
     owner, slot, cols = row_z, row_x, block
 
+    def start(to, col, row, count, lane, width):
+        rs = pl.ds(row, count)
+        src = tiles.at[to, :, rs, pl.ds(pl.multiple_of(col * cols + lane, width), width)]
+        dst = arrived.at[slot, :, rs, pl.ds(pl.multiple_of(core * half + col * cols + lane, width), width)]
+        landing = out_recv.at[slot, core * ROW + col]
+        far = pltpu.make_async_remote_copy(
+            src, dst, out_send, landing, device_id={"freq": plane * CORES + owner, "feed": to}, device_id_type=MESH)
+        near = pltpu.make_async_copy(src, dst, landing)
+        here = jnp.logical_and(to == feed, owner == core)
+
+        @pl.when(here)
+        def _():
+            near.start()
+
+        @pl.when(jnp.logical_not(here))
+        def _():
+            far.start()
+
     def send(to, col):
-        for part in range(2):
-            src = tiles.at[to, part, :, pl.ds(pl.multiple_of(col * cols, cols), cols)]
-            dst = arrived.at[slot, part, :, pl.ds(pl.multiple_of(core * half + col * cols, cols), cols)]
-            far = pltpu.make_async_remote_copy(
-                src, dst, out_send, out_recv.at[slot, core * ROW + col],
-                device_id={"freq": plane * CORES + owner, "feed": to}, device_id_type=MESH)
-            near = pltpu.make_async_copy(src, dst, out_recv.at[slot, core * ROW + col])
-            here = jnp.logical_and(to == feed, owner == core)
-
-            @pl.when(here)
-            def _():
-                near.start()
-
-            @pl.when(jnp.logical_not(here))
-            def _():
-                far.start()
+        diagonal = to == core * ROW + col
+
+        @pl.when(diagonal)
+        def _():
+            start(to, col, 0, cols // 2, 0, cols)
+            start(to, col, cols // 2, cols // 2, cols // 2, cols // 2)
+
+        @pl.when(jnp.logical_not(diagonal))
+        def _():
+            start(to, col, 0, cols, 0, cols)
 
     def correlate(to, col):
         own = samples[pl.ds(pl.multiple_of(to * block, block), block), :]
@@ -217,9 +240,13 @@
         source, f = i // PLACES, i % PLACES
         seen = relayed(far_side, (row_x - source + ROW) % ROW, (f % ROW - source + ROW) % ROW, (f // ROW + core) % 2)
 
-        @pl.when(jnp.logical_not(seen))
+        @pl.when(jnp.logical_not(seen | (f == feed)))
         def _():
             whole(columns(source, f), out_recv.at[source, f]).wait()
+
+        @pl.when(f == feed)
+        def _():
+            whole(tiles.at[0, :, pl.ds(0, cols - cols // 4), pl.ds(0, cols)], out_recv.at[source, f]).wait()
         return carry
 
     lax.fori_loop(0, ROW * PLACES, landed, 0)
@@ -231,7 +258,14 @@
         whole(one_tile, out_send).wait()
         return carry
 
-    lax.fori_loop(0, steps - jnp.where(owner == core, ROW, 0), sent, 0)
+    quarters = 4 * steps - jnp.where(owner == core, 4 * ROW + ROW - 1, ROW)
+    lax.fori_loop(0, quarters // 4, sent, 0)
+
+    def sent_quarter(i, carry):
+        whole(tiles.at[0, :, pl.ds(0, cols // 4), pl.ds(0, cols)], out_send).wait()
+        return carry
+
+    lax.fori_loop(0, quarters % 4, sent_quarter, 0)
 
     def handed(i, carry):
         whole(one_tile, relay_send).wait()
@@ -250,14 +284,23 @@
         at = slice(n * width, (n + 1) * width)
         took = pl.ds(pl.multiple_of(f * width, width), width)
 
+        re, im = (arrived[source, part, :, took].astype(jnp.float32) for part in range(2))
+
         @pl.when(turned)
         def _():
-            out[0, 0, :, at] = arrived[source, 0, :, took].astype(jnp.float32).T
-            out[0, 1, :, at] = -arrived[source, 1, :, took].astype(jnp.float32).T
+            out[0, 0, :, at] = re.T
+            out[0, 1, :, at] = -im.T
 
         @pl.when(jnp.logical_not(turned))
         def _():
-            out[0, :, :, at] = arrived[source, :, :, took].astype(jnp.float32)
+            out[0, 0, :, at] = re
+            out[0, 1, :, at] = im
+
+        @pl.when(f == feed)
+        def _():
+            low, cut = slice(n * width, n * width + width // 2), width // 2
+            out[0, 0, cut:, low] = re[:cut, cut:].T
+            out[0, 1, cut:, low] = -im[:cut, cut:].T
 
 
 def per_device(voltages, gains):

time: 150 us -> 143 us (0.953)
  Pallas kernels: 150 us -> 142 us
    pallas_call x1, Pallas kernels: 142 us -> 134 us  [per_device(): pl.pallas_call(kernel, out_shape=pltpu.VMEM((owned, 2, block, feeds), jnp...]
where the time goes in v5:
time: 143 us
  Pallas kernels  142 us (99%)
    pallas_call x1, Pallas kernels, per_device(): pl.pallas_call(kernel, out_shape=pltpu.VMEM((owned, 2, block, feeds), jnp...  134 us
    pallas_call x1, Pallas kernels, per_device(): pl.pallas_call(finish, out_shape=jax.ShapeDtypeStruct(arrived.shape, jnp....  8.22 us

profile of v5, /device:TPU:1, one launch (start us, length us, event | category | flops | bytes accessed | tf_op | source)
XLA Modules:
  0.0 143.2 jit_solution(5780648690679037062)
XLA Ops:
  0.0 0.0 copy-start
  0.0 0.7 copy-done
  0.7 134.2 %x_engine.1.arrived = bf16[4,2,256,2048]{3,2,1,0:T(8,128)(2,1)S(1)} custom-call(s32[64,16,2,768]{3,2,1,0:T(2,128)} %volt.1, f32[2,16,64]{2,1,0:T(8,128)S(1)} %bitcast.1), custom_call_target="tpu_custom_call" | custom-call | tf_op jit(solution)/shard_map/x_engine/pallas_call | solution.py:311
  134.9 8.2 %widen.1 = f32[4,2,256,2048]{3,2,1,0:T(8,128)} custom-call(bf16[4,2,256,2048]{3,2,1,0:T(8,128)(2,1)S(1)} %x_engine.1.arrived), custom_call_target="tpu_custom_call" | custom-call | tf_op jit(solution)/shard_map/widen/pallas_call | solution.py:334
Async XLA Ops:
  0.0 0.7 copy-start

commit v6 on v5

--- a/solution.py
+++ b/solution.py
@@ -16,8 +16,8 @@
     ((1, 0), (2, 1)), ((1, 1), (2, 1)), ((1, 3), (2, 1)), ((1, 0), (1, 1)), ((1, 0), (3, 1)),
 )
 TILES = (
-    ((1, 0, 2), (3, 0, 2), (0, 1, 0), (1, 1, 0), (3, 1, 0), (2, 0, 0), (1, 0, 0), (3, 0, 0), (0, 1, 1), (1, 1, 2), (3, 1, 1), (2, 1, 0), (1, 0, 1), (3, 0, 1), (0, 1, 2), (2, 0, 2), (1, 1, 3), (3, 1, 2), (1, 0, 3), (3, 0, 3), (0, 1, 3), (0, 0, 0), (0, 0, 1), (0, 0, 2), (0, 0, 3)),
-    ((1, 0, 1), (3, 0, 2), (0, 1, 1), (2, 0, 2), (1, 1, 2), (3, 1, 2), (1, 0, 2), (3, 0, 3), (0, 1, 2), (2, 0, 0), (0, 1, 3), (1, 1, 1), (3, 1, 1), (2, 1, 2), (1, 0, 0), (3, 0, 0), (2, 0, 1), (1, 1, 3), (3, 1, 3), (1, 0, 3), (3, 0, 1), (0, 1, 0), (2, 0, 3), (0, 0, 0), (0, 0, 1), (0, 0, 2), (0, 0, 3)),
+    ((1, 0, 2), (3, 0, 2), (0, 1, 0), (1, 1, 0), (3, 1, 0), (2, 0, 0), (0, 1, 1), (1, 0, 0), (3, 0, 0), (1, 1, 2), (3, 1, 1), (2, 1, 0), (0, 1, 2), (1, 0, 1), (3, 0, 1), (2, 0, 2), (1, 1, 3), (3, 1, 2), (0, 1, 3), (1, 0, 3), (3, 0, 3), (0, 0, 0), (0, 0, 1), (0, 0, 2), (0, 0, 3)),
+    ((0, 1, 1), (1, 0, 1), (3, 0, 2), (2, 0, 2), (1, 1, 2), (3, 1, 2), (0, 1, 2), (1, 0, 2), (3, 0, 3), (2, 0, 0), (0, 1, 3), (1, 1, 1), (3, 1, 1), (2, 1, 2), (1, 0, 0), (3, 0, 0), (2, 0, 1), (1, 1, 3), (3, 1, 3), (0, 1, 0), (1, 0, 3), (3, 0, 1), (2, 0, 3), (0, 0, 0), (0, 0, 1), (0, 0, 2), (0, 0, 3)),
 )
 
 
@@ -52,8 +52,8 @@
 
 
 def offset_of(step):
-    a, b = step // 4 % 4, step % 4
-    return a, b, (step // 16 - a - b + 8) % 4
+    a, b = step % 4, step // 4 % 4
+    return a, (a + step // 16) % 4, (a * 3 + b) % 4
 
 
 def kernel(volt, gains, arrived, raw, eq, samples, tiles, raw_sem, eq_send, eq_recv, pair_send, pair_recv, out_send, out_recv, relay_send):
@@ -229,9 +229,12 @@
         source = (row_x - ax + ROW) % ROW
         to = (core + bz) % 2 * ROW + (source + bx) % ROW
         whole(columns(source, to), out_recv.at[source, to]).wait()
-        pltpu.make_async_remote_copy(
-            columns(source, to), columns(source, feed), relay_send, out_recv.at[source, feed],
-            device_id={"freq": plane * CORES + core, "feed": to}, device_id_type=MESH).start()
+        for part in range(4):
+            rs = pl.ds(part * (cols // 4), cols // 4)
+            pltpu.make_async_remote_copy(
+                arrived.at[source, :, rs, pl.ds(pl.multiple_of(to * cols, cols), cols)],
+                arrived.at[source, :, rs, pl.ds(pl.multiple_of(feed * cols, cols), cols)], relay_send, out_recv.at[source, feed],
+                device_id={"freq": plane * CORES + core, "feed": to}, device_id_type=MESH).start()
         return carry
 
     lax.fori_loop(0, relays, hand_on, 0)
@@ -278,11 +281,11 @@
     _, core, feed = place()
     source, width = pl.program_id(0), out.shape[2]
     for n in range(out.shape[3] // width):
-        f = pl.program_id(1) * (out.shape[3] // width) + n
+        f = n
         turned = relayed((f // ROW + core) % 2, (f % ROW - source + ROW) % ROW,
                          (feed % ROW - source + ROW) % ROW, (feed // ROW + core) % 2)
         at = slice(n * width, (n + 1) * width)
-        took = pl.ds(pl.multiple_of(f * width, width), width)
+        took = at
 
         re, im = (arrived[source, part, :, took].astype(jnp.float32) for part in range(2))
 
@@ -330,14 +333,14 @@
         compiler_params=pltpu.CompilerParams(collective_id=0, has_side_effects=True, vmem_limit_bytes=45 * 2**20),
         name="x_engine",
     )(voltages, gains.transpose(0, 2, 1))
-    spec = pl.BlockSpec((1, 2, block, feeds // 2), lambda i, j: (i, 0, 0, j))
+    spec = pl.BlockSpec((1, 2, block, feeds), lambda i: (i, 0, 0, 0))
     return pl.pallas_call(
         finish,
         out_shape=jax.ShapeDtypeStruct(arrived.shape, jnp.float32),
-        grid=(owned, 2),
+        grid=(owned,),
         in_specs=[pl.BlockSpec(memory_space=pltpu.VMEM)],
         out_specs=spec,
-        compiler_params=pltpu.CompilerParams(vmem_limit_bytes=16 * 2**20),
+        compiler_params=pltpu.CompilerParams(vmem_limit_bytes=24 * 2**20),
         name="widen",
     )(arrived)
 

time: 143 us -> 141 us (0.986)
  Pallas kernels: 142 us -> 139 us
    pallas_call x1, Pallas kernels: 134 us -> 132 us  [per_device(): pl.pallas_call(kernel, out_shape=pltpu.VMEM((owned, 2, block, feeds), jnp...]
where the time goes in v6:
time: 141 us; the launch traced here: 140 us
  Pallas kernels  139 us (99%)
    pallas_call x1, Pallas kernels, per_device(): pl.pallas_call(kernel, out_shape=pltpu.VMEM((owned, 2, block, feeds), jnp...  132 us
    pallas_call x1, Pallas kernels, per_device(): pl.pallas_call(finish, out_shape=jax.ShapeDtypeStruct(arrived.shape, jnp....  7.38 us

profile of v6, /device:TPU:1, one launch (start us, length us, event | category | flops | bytes accessed | tf_op | source)
XLA Modules:
  0.0 140.1 jit_solution(1933805612832865776)
XLA Ops:
  0.0 0.0 copy-start
  0.0 0.7 copy-done
  0.7 132.0 %x_engine.1.arrived = bf16[4,2,256,2048]{3,2,1,0:T(8,128)(2,1)S(1)} custom-call(s32[64,16,2,768]{3,2,1,0:T(2,128)} %volt.1, f32[2,16,64]{2,1,0:T(8,128)S(1)} %bitcast.1), custom_call_target="tpu_custom_call" | custom-call | tf_op jit(solution)/shard_map/x_engine/pallas_call | solution.py:314
  132.8 7.4 %widen.1 = f32[4,2,256,2048]{3,2,1,0:T(8,128)} custom-call(bf16[4,2,256,2048]{3,2,1,0:T(8,128)(2,1)S(1)} %x_engine.1.arrived), custom_call_target="tpu_custom_call" | custom-call | tf_op jit(solution)/shard_map/widen/pallas_call | solution.py:337
Async XLA Ops:
  0.0 0.7 copy-start

commit v7 on v6

--- a/solution.py
+++ b/solution.py
@@ -108,7 +108,7 @@
         eq[pl.ds(step * rows, rows), time:] = (gr * vi + gi * vr).astype(jnp.bfloat16)
         return carry
 
-    lax.fori_loop(0, 24, equalize, 0)
+    lax.fori_loop(0, 16, equalize, 0)
     pl.semaphore_wait(barrier, chans - 1 + PLACES)
     own_copy.start()
 
@@ -116,18 +116,17 @@
         eq_copy(step).start()
         return carry
 
-    lax.fori_loop(1, 24, send_eq, 0)
+    lax.fori_loop(1, 16, send_eq, 0)
 
     def equalize_and_send(step, carry):
         equalize(step, carry)
 
-        @pl.when(step > 24)
+        @pl.when(step > 16)
         def _():
             eq_copy(step - 1).start()
         return carry
 
-    lax.fori_loop(24, chans, equalize_and_send, 0)
-    eq_copy(chans - 1).start()
+    lax.fori_loop(16, chans, equalize_and_send, 0)
 
     def pair_copy(f, p):
         at = f * block + (p * CORES + core) * rows
@@ -203,7 +202,6 @@
             return carry
 
         lax.fori_loop(0, steps, one, 0)
-        send(*tile(steps - 1))
 
     far_side = (core + row_z) % 2
     steps = len(TILES[0]) + far_side * (len(TILES[1]) - len(TILES[0]))
@@ -213,7 +211,9 @@
         dx, dz, col = (jnp.where(far_side == 1, v, u) for u, v in zip(close, far))
         return near_place(dx, dz), (row_x + col) % ROW
 
-    lax.fori_loop(0, chans, pass_on, 0)
+    pass_on(0, 0)
+    eq_copy(chans - 1).start()
+    lax.fori_loop(1, chans, pass_on, 0)
     whole(samples.at[pl.ds(0, half)], pair_recv).wait()
     tile_loop(steps, tile)
 
@@ -238,6 +238,7 @@
         return carry
 
     lax.fori_loop(0, relays, hand_on, 0)
+    send(*tile(steps - 1))
 
     def landed(i, carry):
         source, f = i // PLACES, i % PLACES

time: 141 us -> 140 us (level)
  no operation moved by 1% of the time
where the time goes in v7:
time: 140 us
  Pallas kernels  139 us (99%)
    pallas_call x1, Pallas kernels, per_device(): pl.pallas_call(kernel, out_shape=pltpu.VMEM((owned, 2, block, feeds), jnp...  132 us
    pallas_call x1, Pallas kernels, per_device(): pl.pallas_call(finish, out_shape=jax.ShapeDtypeStruct(arrived.shape, jnp....  7.38 us

profile of v7, /device:TPU:1, one launch (start us, length us, event | category | flops | bytes accessed | tf_op | source)
XLA Modules:
  0.0 139.8 jit_solution(10738366170914484381)
XLA Ops:
  0.0 0.0 copy-start
  0.0 0.7 copy-done
  0.7 131.7 %x_engine.1.arrived = bf16[4,2,256,2048]{3,2,1,0:T(8,128)(2,1)S(1)} custom-call(s32[64,16,2,768]{3,2,1,0:T(2,128)} %volt.1, f32[2,16,64]{2,1,0:T(8,128)S(1)} %bitcast.1), custom_call_target="tpu_custom_call" | custom-call | tf_op jit(solution)/shard_map/x_engine/pallas_call | solution.py:315
  132.4 7.4 %widen.1 = f32[4,2,256,2048]{3,2,1,0:T(8,128)} custom-call(bf16[4,2,256,2048]{3,2,1,0:T(8,128)(2,1)S(1)} %x_engine.1.arrived), custom_call_target="tpu_custom_call" | custom-call | tf_op jit(solution)/shard_map/widen/pallas_call | solution.py:338
Async XLA Ops:
  0.0 0.7 copy-start
